TPU v7x, 32 devices: a whole 2x2x4 slice. The times are simulated.
32 devices in a mesh: fsdp: 16 (over z, x, core), tp: 2 (over y).
Axes of the slice: x: 2, y: 2, z: 4, core: 2. Of those that a mesh axis runs over, the one named last changes fastest.
Arguments:
- block_input: bfloat16 [3072, 2304], P(('fsdp', 'tp')), may hold values from -6 to 6
- lengths: int32 [16, 9], P('fsdp'), may hold values from 1 to 96, 192 in all within a row
- attention_norm_gain: bfloat16 [2304], P('fsdp'), may hold values from 0.25 to 1.75
- attention_post_gain: bfloat16 [2304], P('fsdp'), may hold values from 0.25 to 1.75
- feedforward_norm_gain: bfloat16 [2304], P('fsdp'), may hold values from 0.25 to 1.75
- feedforward_post_gain: bfloat16 [2304], P('fsdp'), may hold values from 0.25 to 1.75
- query_weight: bfloat16 [2304, 2048], P('fsdp', 'tp'), may hold values from -0.125 to 0.125
- key_weight: bfloat16 [2304, 1024], P('fsdp', 'tp'), may hold values from -0.125 to 0.125
- value_weight: bfloat16 [2304, 1024], P('fsdp', 'tp'), may hold values from -0.125 to 0.125
- output_weight: bfloat16 [2304, 2048], P('fsdp', 'tp'), may hold values from -0.125 to 0.125
- gate_weight: bfloat16 [2304, 9216], P('fsdp', 'tp'), may hold values from -0.125 to 0.125
- up_weight: bfloat16 [2304, 9216], P('fsdp', 'tp'), may hold values from -0.125 to 0.125
- down_weight: bfloat16 [2304, 9216], P('fsdp', 'tp'), may hold values from -0.0625 to 0.0625
- output_cotangent: bfloat16 [3072, 2304], P(('fsdp', 'tp')), may hold values from -6 to 6
Outputs:
- block_output: bfloat16 [3072, 2304], P(('fsdp', 'tp'))
- input_gradient: float32 [3072, 2304], P(('fsdp', 'tp'))
- attention_norm_gain_gradient: float32 [2304], P('fsdp')
- attention_post_gain_gradient: float32 [2304], P('fsdp')
- feedforward_norm_gain_gradient: float32 [2304], P('fsdp')
- feedforward_post_gain_gradient: float32 [2304], P('fsdp')
- query_weight_gradient: float32 [2304, 2048], P('fsdp', 'tp')
- key_weight_gradient: float32 [2304, 1024], P('fsdp', 'tp')
- value_weight_gradient: float32 [2304, 1024], P('fsdp', 'tp')
- output_weight_gradient: float32 [2304, 2048], P('fsdp', 'tp')
- gate_weight_gradient: float32 [2304, 9216], P('fsdp', 'tp')
- up_weight_gradient: float32 [2304, 9216], P('fsdp', 'tp')
- down_weight_gradient: float32 [2304, 9216], P('fsdp', 'tp')
Inputs may be any that keep to these rules, and one draw needn't show every extreme that they name: `lengths`: row g gives the length of group g's prompt (column 0) and of its 8 continuations; each row sums to 192, and its largest entry is 96.
All inputs are finite; a program needn't handle non-finite values.
Results may differ from a plain program's by a relative error of at most 0.017.
Values may be sent and summed in bfloat16 or wider, within the bound.
A program may use at most 512 MiB of HBM per device.

v0:
```python
import math
import jax
import jax.numpy as jnp
from jax import lax
from jax.sharding import PartitionSpec as P

HEAD_SIZE = 256
EPSILON = 1e-06
SOFTCAP = 50.0
NEGATIVE = -1e30


def contract_last(left_rows, right_rows):
    return lax.dot_general(
        left_rows, right_rows, (((1,), (1,)), ((), ())), preferred_element_type=jnp.float32
    )


def contract_first(left_rows, right_rows):
    return lax.dot_general(
        left_rows, right_rows, (((0,), (0,)), ((), ())), preferred_element_type=jnp.float32
    )


def normalize_parts(value_rows):
    inverse = lax.rsqrt(jnp.mean(value_rows * value_rows, axis=-1, keepdims=True) + EPSILON)
    return (value_rows * inverse, inverse)


def norm_backward(unit_rows, inverse, norm_gain, upstream):
    scaled = upstream * norm_gain
    return inverse * (scaled - unit_rows * jnp.mean(scaled * unit_rows, axis=-1, keepdims=True))


def layout(lengths_row, grouped_rows):
    segment_ends = jnp.cumsum(lengths_row)
    segment_starts = segment_ends - lengths_row
    row_index = jnp.arange(grouped_rows, dtype=jnp.int32)
    segment = jnp.sum((row_index[:, None] >= segment_ends[None, :]).astype(jnp.int32), axis=1)
    onehot = segment[:, None] == jnp.arange(lengths_row.shape[0], dtype=jnp.int32)[None, :]
    segment_begin = jnp.sum(jnp.where(onehot, segment_starts[None, :], 0), axis=1)
    prompt_shift = jnp.where(segment > 0, lengths_row[0], 0)
    return (segment, row_index - segment_begin + prompt_shift)


def rotary_tables(position):
    frequency = jnp.exp(
        jnp.arange(HEAD_SIZE // 2, dtype=jnp.float32) * (-2.0 * math.log(10000.0) / HEAD_SIZE)
    )
    angles = position.astype(jnp.float32)[:, None] * frequency[None, :]
    return (jnp.cos(angles), jnp.sin(angles))


def apply_rotary(value_rows, cosine_lookup, sine_lookup):
    half_width = value_rows.shape[-1] // 2
    first_half = value_rows[..., :half_width]
    second_half = value_rows[..., half_width:]
    cosine_part = cosine_lookup[:, None, :]
    sine_part = sine_lookup[:, None, :]
    return jnp.concatenate(
        [
            first_half * cosine_part - second_half * sine_part,
            second_half * cosine_part + first_half * sine_part,
        ],
        axis=-1,
    )


def unrotate(value_rows, cosine_lookup, sine_lookup):
    half_width = value_rows.shape[-1] // 2
    first_half = value_rows[..., :half_width]
    second_half = value_rows[..., half_width:]
    cosine_part = cosine_lookup[:, None, :]
    sine_part = sine_lookup[:, None, :]
    return jnp.concatenate(
        [
            first_half * cosine_part + second_half * sine_part,
            second_half * cosine_part - first_half * sine_part,
        ],
        axis=-1,
    )


def visible(segment):
    row_index = jnp.arange(segment.shape[0], dtype=jnp.int32)
    same_segment = (segment[:, None] == segment[None, :]) & (
        row_index[None, :] <= row_index[:, None]
    )
    from_prompt = (segment[None, :] == 0) & (segment[:, None] > 0)
    return same_segment | from_prompt


def masked_scores(rotated_query, rotated_key, visible_mask):
    raw_scores = jnp.einsum(
        "qgrd,kgd->grqk", rotated_query, rotated_key, preferred_element_type=jnp.float32
    )
    tanh_value = jnp.tanh(raw_scores * HEAD_SIZE ** (-0.5) / SOFTCAP)
    return (jnp.where(visible_mask[None, None], SOFTCAP * tanh_value, NEGATIVE), tanh_value)


def gelu_product(gate_value, up_value):
    return jax.nn.gelu(gate_value, approximate=True) * up_value


def shards(
    block_input,
    lengths,
    attention_norm_gain,
    attention_post_gain,
    feedforward_norm_gain,
    feedforward_post_gain,
    query_weight,
    key_weight,
    value_weight,
    output_weight,
    gate_weight,
    up_weight,
    down_weight,
    output_cotangent,
):
    query_full, key_full, value_full, output_full, gain_one, gain_two = (
        lax.all_gather(query_weight, "fsdp", axis=0, tiled=True),
        lax.all_gather(key_weight, "fsdp", axis=0, tiled=True),
        lax.all_gather(value_weight, "fsdp", axis=0, tiled=True),
        lax.all_gather(output_weight, "fsdp", axis=0, tiled=True),
        lax.all_gather(attention_norm_gain, "fsdp", axis=0, tiled=True),
        lax.all_gather(attention_post_gain, "fsdp", axis=0, tiled=True),
    )
    gate_full, up_full, down_full, gain_three, gain_four = (
        lax.all_gather(gate_weight, "fsdp", axis=0, tiled=True),
        lax.all_gather(up_weight, "fsdp", axis=0, tiled=True),
        lax.all_gather(down_weight, "fsdp", axis=0, tiled=True),
        lax.all_gather(feedforward_norm_gain, "fsdp", axis=0, tiled=True),
        lax.all_gather(feedforward_post_gain, "fsdp", axis=0, tiled=True),
    )
    gain_one = gain_one.astype(jnp.float32)
    gain_two = gain_two.astype(jnp.float32)
    gain_three = gain_three.astype(jnp.float32)
    gain_four = gain_four.astype(jnp.float32)
    rows_local = block_input.shape[0]
    grouped_rows = rows_local * lax.axis_size("tp")
    segment, position = layout(lengths[0], grouped_rows)
    cosine_lookup, sine_lookup = rotary_tables(position)
    visible_mask = visible(segment)
    residual = block_input.astype(jnp.float32)
    unit_one, inverse_one = normalize_parts(residual)
    normed_local = (unit_one * gain_one).astype(jnp.bfloat16)
    normed = lax.all_gather(normed_local, "tp", axis=0, tiled=True)
    query_raw = jnp.dot(normed, query_full, preferred_element_type=jnp.float32)
    key_raw = jnp.dot(normed, key_full, preferred_element_type=jnp.float32)
    value_raw = jnp.dot(normed, value_full, preferred_element_type=jnp.float32)
    heads_local = query_raw.shape[1] // HEAD_SIZE
    kv_local = key_raw.shape[1] // HEAD_SIZE
    repeat_heads = heads_local // kv_local
    rotated_query = apply_rotary(
        query_raw.reshape(grouped_rows, heads_local, HEAD_SIZE), cosine_lookup, sine_lookup
    ).astype(jnp.bfloat16)
    rotated_query = rotated_query.reshape(grouped_rows, kv_local, repeat_heads, HEAD_SIZE)
    rotated_key = apply_rotary(
        key_raw.reshape(grouped_rows, kv_local, HEAD_SIZE), cosine_lookup, sine_lookup
    ).astype(jnp.bfloat16)
    value_reduced = value_raw.astype(jnp.bfloat16).reshape(grouped_rows, kv_local, HEAD_SIZE)
    capped, tanh_value = masked_scores(rotated_query, rotated_key, visible_mask)
    row_peak = jnp.max(capped, axis=-1, keepdims=True)
    log_total = row_peak + jnp.log(jnp.sum(jnp.exp(capped - row_peak), axis=-1, keepdims=True))
    softmax_probs = jnp.exp(capped - log_total)
    mixed_heads = jnp.einsum(
        "grqk,kgd->qgrd",
        softmax_probs.astype(jnp.bfloat16),
        value_reduced,
        preferred_element_type=jnp.float32,
    )
    attended = mixed_heads.reshape(grouped_rows, heads_local * HEAD_SIZE).astype(jnp.bfloat16)
    row_piece = attended
    branch_one = lax.psum_scatter(
        contract_last(row_piece, output_full), "tp", scatter_dimension=0, tiled=True
    )
    unit_two, inverse_two = normalize_parts(branch_one)
    middle = residual + unit_two * gain_two
    unit_three, inverse_three = normalize_parts(middle)
    feed_local = (unit_three * gain_three).astype(jnp.bfloat16)
    feed_input = lax.all_gather(feed_local, "tp", axis=0, tiled=True)
    gate_value = jnp.dot(feed_input, gate_full, preferred_element_type=jnp.float32)
    up_value = jnp.dot(feed_input, up_full, preferred_element_type=jnp.float32)
    hidden = gelu_product(gate_value, up_value).astype(jnp.bfloat16)
    row_piece = hidden
    branch_two = lax.psum_scatter(
        contract_last(row_piece, down_full), "tp", scatter_dimension=0, tiled=True
    )
    unit_four, inverse_four = normalize_parts(branch_two)
    block_output = (middle + unit_four * gain_four).astype(jnp.bfloat16)
    upstream = output_cotangent.astype(jnp.float32)
    gain_four_grad = jnp.sum(upstream * unit_four, axis=0)
    branch_two_grad = norm_backward(unit_four, inverse_four, gain_four, upstream).astype(
        jnp.bfloat16
    )
    held_back = lax.optimization_barrier(
        (
            query_weight,
            key_weight,
            value_weight,
            output_weight,
            gate_weight,
            up_weight,
            down_weight,
            branch_two_grad,
        )
    )
    query_full, key_full, value_full, output_full, gate_full, up_full, down_full = (
        lax.all_gather(held_back[0], "fsdp", axis=0, tiled=True),
        lax.all_gather(held_back[1], "fsdp", axis=0, tiled=True),
        lax.all_gather(held_back[2], "fsdp", axis=0, tiled=True),
        lax.all_gather(held_back[3], "fsdp", axis=0, tiled=True),
        lax.all_gather(held_back[4], "fsdp", axis=0, tiled=True),
        lax.all_gather(held_back[5], "fsdp", axis=0, tiled=True),
        lax.all_gather(held_back[6], "fsdp", axis=0, tiled=True),
    )
    branch_two_grad = held_back[7]
    feed_grad_rows = lax.all_gather(branch_two_grad, "tp", axis=0, tiled=True)
    hidden_grad = jnp.dot(feed_grad_rows, down_full, preferred_element_type=jnp.float32)
    unused_out, pullback = jax.vjp(gelu_product, gate_value, up_value)
    gate_grad, up_grad = pullback(hidden_grad)
    gate_up_grad = jnp.concatenate(
        [gate_grad.astype(jnp.bfloat16), up_grad.astype(jnp.bfloat16)], axis=1
    )
    feed_split = gate_full.shape[1]
    shard_rows = query_weight.shape[0]
    left_rows = feed_input
    feed_weight_grads = lax.psum_scatter(
        jnp.concatenate(
            [contract_first(left_rows, gate_up_grad), contract_first(feed_grad_rows, hidden)],
            axis=1,
        ),
        "fsdp",
        scatter_dimension=0,
        tiled=True,
    )
    row_piece = gate_up_grad
    normed_three_grad = lax.psum_scatter(
        contract_last(row_piece[:, :feed_split], gate_full)
        + contract_last(row_piece[:, feed_split:], up_full),
        "tp",
        scatter_dimension=0,
        tiled=True,
    )
    gain_three_grad = jnp.sum(normed_three_grad * unit_three, axis=0)
    middle_grad = upstream + norm_backward(unit_three, inverse_three, gain_three, normed_three_grad)
    gain_two_grad = jnp.sum(middle_grad * unit_two, axis=0)
    branch_one_grad = norm_backward(unit_two, inverse_two, gain_two, middle_grad).astype(
        jnp.bfloat16
    )
    attention_grad_rows = lax.all_gather(branch_one_grad, "tp", axis=0, tiled=True)
    mixed_grad = jnp.dot(
        attention_grad_rows, output_full, preferred_element_type=jnp.float32
    ).astype(jnp.bfloat16)
    mixed_grad = mixed_grad.reshape(grouped_rows, kv_local, repeat_heads, HEAD_SIZE)
    capped_again, tanh_again = masked_scores(rotated_query, rotated_key, visible_mask)
    probs_again = jnp.exp(capped_again - log_total)
    value_grad = jnp.einsum(
        "grqk,qgrd->kgd",
        probs_again.astype(jnp.bfloat16),
        mixed_grad,
        preferred_element_type=jnp.float32,
    )
    probs_grad = jnp.einsum(
        "qgrd,kgd->grqk", mixed_grad, value_reduced, preferred_element_type=jnp.float32
    )
    score_grad = probs_again * (
        probs_grad - jnp.sum(probs_again * probs_grad, axis=-1, keepdims=True)
    )
    raw_grad = (score_grad * (1.0 - tanh_again * tanh_again) * HEAD_SIZE ** (-0.5)).astype(
        jnp.bfloat16
    )
    query_grad = jnp.einsum(
        "grqk,kgd->qgrd", raw_grad, rotated_key, preferred_element_type=jnp.float32
    )
    key_grad = jnp.einsum(
        "grqk,qgrd->kgd", raw_grad, rotated_query, preferred_element_type=jnp.float32
    )
    query_grad = unrotate(
        query_grad.reshape(grouped_rows, heads_local, HEAD_SIZE), cosine_lookup, sine_lookup
    )
    key_grad = unrotate(key_grad, cosine_lookup, sine_lookup)
    projected_grad = jnp.concatenate(
        [
            query_grad.reshape(grouped_rows, heads_local * HEAD_SIZE).astype(jnp.bfloat16),
            key_grad.reshape(grouped_rows, kv_local * HEAD_SIZE).astype(jnp.bfloat16),
            value_grad.reshape(grouped_rows, kv_local * HEAD_SIZE).astype(jnp.bfloat16),
        ],
        axis=1,
    )
    query_width = query_full.shape[1]
    key_width = key_full.shape[1]
    left_rows = normed
    attention_weight_grads = lax.psum_scatter(
        jnp.concatenate(
            [
                contract_first(left_rows, projected_grad),
                contract_first(attention_grad_rows, attended),
            ],
            axis=1,
        ),
        "fsdp",
        scatter_dimension=0,
        tiled=True,
    )
    row_piece = projected_grad
    total = contract_last(row_piece[:, :query_width], query_full)
    total = total + contract_last(row_piece[:, query_width : query_width + key_width], key_full)
    normed_one_grad = lax.psum_scatter(
        (total + contract_last(row_piece[:, query_width + key_width :], value_full)).astype(
            jnp.bfloat16
        ),
        "tp",
        scatter_dimension=0,
        tiled=True,
    ).astype(jnp.float32)
    gain_one_grad = jnp.sum(normed_one_grad * unit_one, axis=0)
    input_gradient = middle_grad + norm_backward(unit_one, inverse_one, gain_one, normed_one_grad)
    gain_sums = lax.psum(
        (gain_one_grad, gain_two_grad, gain_three_grad, gain_four_grad), ("fsdp", "tp")
    )
    offset = lax.axis_index("fsdp") * shard_rows
    gain_shards = [
        lax.dynamic_slice_in_dim(total_sum, offset, shard_rows) for total_sum in gain_sums
    ]
    value_start = query_width + key_width
    output_start = value_start + key_width
    return (
        block_output,
        input_gradient,
        gain_shards[0],
        gain_shards[1],
        gain_shards[2],
        gain_shards[3],
        attention_weight_grads[:, :query_width],
        attention_weight_grads[:, query_width:value_start],
        attention_weight_grads[:, value_start:output_start],
        attention_weight_grads[:, output_start:],
        feed_weight_grads[:, :feed_split],
        feed_weight_grads[:, feed_split : 2 * feed_split],
        feed_weight_grads[:, 2 * feed_split :],
    )


def solution(mesh):
    placed = (
        P(("fsdp", "tp"), None),
        P("fsdp", None),
        P("fsdp"),
        P("fsdp"),
        P("fsdp"),
        P("fsdp"),
        P("fsdp", "tp"),
        P("fsdp", "tp"),
        P("fsdp", "tp"),
        P("fsdp", "tp"),
        P("fsdp", "tp"),
        P("fsdp", "tp"),
        P("fsdp", "tp"),
        P(("fsdp", "tp"), None),
    )
    return jax.shard_map(
        shards,
        mesh=mesh,
        in_specs=placed,
        out_specs=(
            P(("fsdp", "tp"), None),
            P(("fsdp", "tp"), None),
            P("fsdp"),
            P("fsdp"),
            P("fsdp"),
            P("fsdp"),
            P("fsdp", "tp"),
            P("fsdp", "tp"),
            P("fsdp", "tp"),
            P("fsdp", "tp"),
            P("fsdp", "tp"),
            P("fsdp", "tp"),
            P("fsdp", "tp"),
        ),
        check_vma=False,
    )
```

profile of v0, /device:TPU:0, one launch (start us, length us, event | category | flops | bytes accessed | tf_op | source)
XLA Modules:
  0.0 2708.5 jit_solution(12363852051479386329)
XLA Ops:
  10.0 1.2 dynamic-slice
  15.4 63.9 %all-reduce.5 = (bf16[2304]{0:T(1024)(128)(2,1)S(1)}, bf16[2304]{0:T(1024)(128)(2,1)S(1)}, bf16[2304]{0:T(1024)(128)(2,1)S(1)}, bf16[2304]{0:T(1024)(128)(2,1)S(1)}) all-reduce(bf16[2304]{0:T(1024)(128)(2,1)S(1)} %dynamic-update-slice, bf16[2304]{0:T(1024)(128)(2,1)S(1)} %dynamic-update-slice.1, ...), channel_id=1, replica_groups=mesh['fsdp'=16,'tp'=2] {'fsdp'}, use_global_device_ids=true, to_apply=%add | all-reduce | flops 9216 | bytes 36864
  80.9 1.2 fusion.37
  82.1 1.2 fusion.34
  83.3 9.0 all_gather.67
  93.0 2.3 fusion.107
  95.6 3.4 all-gather.15.cloned.1.call-done
  99.0 2.3 convolution_convert_fusion.2
  101.6 51.6 %all-gather.19.cloned.1.call-done = bf16[2304,1024]{1,0:T(8,128)(2,1)} async-done(((bf16[144,1024]{1,0:T(8,128)(2,1)}), bf16[2304,1024]{1,0:T(8,128)(2,1)}) %all-gather.19.cloned.1.call-update) | async-done | bytes 4718608 | tf_op jit(solution)/shard_map/all_gather | solution.py:122
  153.2 3.4 fusion.108
  159.3 47.7 %all-gather.21.cloned.1.call-done = bf16[2304,1024]{1,0:T(8,128)(2,1)} async-done(((bf16[144,1024]{1,0:T(8,128)(2,1)}), bf16[2304,1024]{1,0:T(8,128)(2,1)}) %all-gather.21.cloned.1.call-update) | async-done | bytes 4718608 | tf_op jit(solution)/shard_map/all_gather | solution.py:125
  207.0 5.2 fusion.109
  214.4 24.9 reduce-scatter.9.cloned.1.call-done
  239.3 1.3 multiply_reduce_fusion.6
  240.6 1.5 multiply_reduce_fusion.5
  242.3 12.7 all_gather.74
  255.1 95.7 %all-gather.23.cloned.1.call-done = bf16[2304,4608]{1,0:T(8,128)(2,1)} async-done(((bf16[144,4608]{1,0:T(8,128)(2,1)}), bf16[2304,4608]{1,0:T(8,128)(2,1)}) %all-gather.23.cloned.1.call-update) | async-done | bytes 21233680 | tf_op jit(solution)/shard_map/all_gather | solution.py:130
  350.8 11.4 fusion.110
  362.2 100.3 %all-gather.25.cloned.1.call-done = bf16[2304,4608]{1,0:T(8,128)(2,1)} async-done(((bf16[144,4608]{1,0:T(8,128)(2,1)}), bf16[2304,4608]{1,0:T(8,128)(2,1)}) %all-gather.25.cloned.1.call-update) | async-done | bytes 21233680 | tf_op jit(solution)/shard_map/all_gather | solution.py:131
  462.4 14.7 multiply_convert_fusion.1
  477.2 96.9 %all-gather.27.cloned.1.call-done = bf16[2304,4608]{1,0:T(8,128)(2,1)} async-done(((bf16[144,4608]{1,0:T(8,128)(2,1)}), bf16[2304,4608]{1,0:T(8,128)(2,1)}) %all-gather.27.cloned.1.call-update) | async-done | bytes 21233680 | tf_op jit(solution)/shard_map/all_gather | solution.py:132
  574.0 12.6 fusion.111
  586.8 28.4 %reduce-scatter.11.cloned.1.call-done = f32[96,2304]{1,0:T(8,128)} async-done(((f32[192,2304]{1,0:T(8,128)}), f32[96,2304]{1,0:T(8,128)}) %reduce-scatter.11.cloned.1.call-update) | async-done | bytes 884752 | tf_op jit(solution)/shard_map/reduce_scatter | solution.py:187
  615.1 1.3 multiply_reduce_fusion.4
  616.5 2.0 fusion.38
  618.5 2.2 fusion.31
  622.2 12.9 all_gather.79
  635.1 95.9 %all-gather.29.cloned.1.call-done = bf16[2304,4608]{1,0:T(8,128)(2,1)} async-done(((bf16[144,4608]{1,0:T(8,128)(2,1)}), bf16[2304,4608]{1,0:T(8,128)(2,1)}) %all-gather.29.cloned.1.call-update) | async-done | bytes 21233680 | tf_op jit(solution)/shard_map/all_gather | solution.py:216
  731.0 14.2 multiply_convert_fusion
  745.2 97.4 %all-gather.31.cloned.1.call-done = bf16[2304,4608]{1,0:T(8,128)(2,1)} async-done(((bf16[144,4608]{1,0:T(8,128)(2,1)}), bf16[2304,4608]{1,0:T(8,128)(2,1)}) %all-gather.31.cloned.1.call-update) | async-done | bytes 21233680 | tf_op jit(solution)/shard_map/all_gather | solution.py:214
  842.6 12.6 fusion.112
  855.2 98.8 %all-gather.33.cloned.1.call-done = bf16[2304,4608]{1,0:T(8,128)(2,1)} async-done(((bf16[144,4608]{1,0:T(8,128)(2,1)}), bf16[2304,4608]{1,0:T(8,128)(2,1)}) %all-gather.33.cloned.1.call-update) | async-done | bytes 21233680 | tf_op jit(solution)/shard_map/all_gather | solution.py:215
  954.1 13.1 convolution_add_fusion.2
  969.6 26.1 reduce-scatter.13.cloned.1.call-done
  995.7 2.0 multiply_reduce_fusion
  997.7 2.2 multiply_reduce_fusion.1
  1000.8 12.6 all_gather.83
  1013.4 37.5 %all-gather.35.cloned.1.call-done = bf16[2304,1024]{1,0:T(8,128)(2,1)} async-done(((bf16[144,1024]{1,0:T(8,128)(2,1)}), bf16[2304,1024]{1,0:T(8,128)(2,1)}) %all-gather.35.cloned.1.call-update) | async-done | bytes 4718608 | tf_op jit(solution)/shard_map/all_gather | solution.py:213
  1051.0 4.2 convolution_convert_fusion
  1055.1 1.3 reshape.272
  1057.6 1.2 convolution_bitcast_fusion
  1058.8 2.3 convolution_bitcast_fusion.2
  1061.9 3.1 fusion.39
  1067.1 37.7 %all-gather.37.cloned.1.call-done = bf16[2304,1024]{1,0:T(8,128)(2,1)} async-done(((bf16[144,1024]{1,0:T(8,128)(2,1)}), bf16[2304,1024]{1,0:T(8,128)(2,1)}) %all-gather.37.cloned.1.call-update) | async-done | bytes 4718608 | tf_op jit(solution)/shard_map/all_gather | solution.py:210
  1104.8 5.3 fusion.113
  1110.1 37.7 %all-gather.39.cloned.1.call-done = bf16[2304,512]{1,0:T(8,128)(2,1)} async-done(((bf16[144,512]{1,0:T(8,128)(2,1)}), bf16[2304,512]{1,0:T(8,128)(2,1)}) %all-gather.39.cloned.1.call-update) | async-done | bytes 2359312 | tf_op jit(solution)/shard_map/all_gather | solution.py:211
  1147.8 3.2 convolution_add_fusion.1
  1151.1 5.0 fusion.114
  1156.1 8.0 fusion.44
  1164.1 26.9 all-gather.41.cloned.1.call-done
  1191.0 3.5 fusion.1
  1194.6 18.8 pad_maximum_fusion.1
  1213.4 27.7 %copy.111 = f32[2304,3072]{1,0:T(8,128)} copy(f32[2304,3072]{0,1:T(8,128)} %pad_maximum_fusion.1) | data formatting | bytes 56623104
  1242.3 27.8 %fusion.115 = f32[2304,4608]{1,0:T(8,128)} fusion(bf16[192,2304]{1,0:T(8,128)(2,1)S(1)} %copy-done.6, bf16[192,4608]{1,0:T(8,128)(2,1)} %get-tuple-element.129), kind=kOutput, calls=%fused_computation.171 | convolution fusion | flops 4076863488 | bytes 45121536 | tf_op jit(solution)/shard_map/dot_general | solution.py:20
  1270.1 32.5 %fusion.9 = f32[2304,9216]{1,0:T(8,128)} fusion(bf16[192,2304]{1,0:T(8,128)(2,1)S(1)} %copy-done.9, bf16[192,4608]{1,0:T(8,128)(2,1)S(1)} %copy-done.17, bf16[192,4608]{1,0:T(8,128)(2,1)S(1)} %copy-done.18), kind=kOutput, calls=%fused_computation.16 | convolution fusion | flops 8160804864 | bytes 89358336 | tf_op jit(solution)/shard_map/dot_general | solution.py:20
  1302.7 85.6 %pad_maximum_fusion = f32[2304,13824]{1,0:T(8,128)} fusion(f32[2304,4608]{1,0:T(8,128)} %fusion.115, f32[2304,9216]{1,0:T(8,128)} %fusion.9), kind=kLoop, calls=%fused_computation.1 | loop fusion | flops 31850496 | bytes 254803968 | tf_op jit(solution)/shard_map/concatenate | solution.py:230
  1389.3 1.4 fusion.36
  1390.7 40.4 %all-reduce.4 = (f32[2304]{0:T(1024)S(1)}, f32[2304]{0:T(1024)S(1)}, f32[2304]{0:T(1024)S(1)}, f32[2304]{0:T(1024)S(1)}) all-reduce(f32[2304]{0:T(1024)S(1)} %get-tuple-element.87, f32[2304]{0:T(1024)S(1)} %copy-done.40, f32[2304]{0:T(1024)S(1)} %copy-done.39, f32[2304]{0:T(1024)S(1)} %copy-done.38), channel_id=1, replica_groups=mesh['fsdp'=16,'tp'=2] {'fsdp','tp'}, use_global_device_ids=true, to_apply=%region_19.20 | all-reduce | flops 9216 | bytes 73728 | tf_op jit(solution)/shard_map/psum | solution.py:320
  1433.7 2.2 fusion.33
  1436.0 76.9 %reduce-scatter.19.cloned.1.call-done = f32[144,3072]{1,0:T(8,128)} async-done(((f32[2304,3072]{1,0:T(8,128)}), f32[144,3072]{1,0:T(8,128)}) %reduce-scatter.19.cloned.1.call-update) | async-done | bytes 1769488
  1512.9 1.9 fusion.104
  1514.8 2.4 fusion.103
  1517.2 1177.5 %reduce-scatter.17.cloned.1.call-done = f32[144,13824]{1,0:T(8,128)} async-done(((f32[2304,13824]{1,0:T(8,128)}), f32[144,13824]{1,0:T(8,128)}) %reduce-scatter.17.cloned.1.call-update) | async-done | bytes 7962640 | tf_op jit(solution)/shard_map/reduce_scatter | solution.py:229
  2694.7 6.8 fusion.102
  (196 shorter events, 27.1 us)
Async XLA Ops:
  7.2 85.1 %copy-start.47 = (s32[1,9]{1,0:T(1,128)S(1)}, s32[1,9]{1,0:T(1,128)}, u32[]{:S(2)}) copy-start(s32[1,9]{1,0:T(1,128)} %param.15) | copy-start | bytes 112
  7.2 85.8 %all-gather.17.cloned.1.call-start = ((), (), s32[]{:S(2)}) async-start(), calls=%async_computation.7 | async-start | bytes 2506752 | tf_op jit(solution)/shard_map/all_gather | solution.py:123
  7.9 91.1 %all-gather.15.cloned.1.call-start = ((), (), s32[]{:S(2)}) async-start(), calls=%async_computation.6 | async-start | bytes 2506752 | tf_op jit(solution)/shard_map/all_gather | solution.py:124
  8.7 144.5 %all-gather.19.cloned.1.call-start = ((), (), s32[]{:S(2)}) async-start(), calls=%async_computation.8 | async-start | bytes 5013504 | tf_op jit(solution)/shard_map/all_gather | solution.py:122
  9.4 197.6 %all-gather.21.cloned.1.call-start = ((), (), s32[]{:S(2)}) async-start(), calls=%async_computation.9 | async-start | bytes 5013504 | tf_op jit(solution)/shard_map/all_gather | solution.py:125
  10.0 229.3 %reduce-scatter.9.cloned.1.call-start = ((), (), s32[]{:S(2)}) async-start(), calls=%async_computation.10 | async-start | bytes 2654208 | tf_op jit(solution)/shard_map/reduce_scatter | solution.py:175
  79.2 13.7 copy-start.27
  82.1 13.4 copy-start.41
  92.5 65.4 %copy-start.29 = (pred[192,192]{0,1:T(8,128)(4,1)}, pred[192,192]{0,1:T(8,128)(4,1)S(1)}, u32[]{:S(2)}) copy-start(pred[192,192]{0,1:T(8,128)(4,1)S(1)} %fusion.77) | copy-start | bytes 110596
  92.9 64.0 %copy-start.10 = (f32[192,128]{1,0:T(8,128)}, f32[192,128]{1,0:T(8,128)S(1)}, u32[]{:S(2)}) copy-start(f32[192,128]{1,0:T(8,128)S(1)} %get-tuple-element.125) | copy-start | bytes 294916
  92.9 64.0 %copy-start.12 = (f32[192,128]{1,0:T(8,128)}, f32[192,128]{1,0:T(8,128)S(1)}, u32[]{:S(2)}) copy-start(f32[192,128]{1,0:T(8,128)S(1)} %get-tuple-element.126) | copy-start | bytes 294916
  101.3 56.6 %copy-start.25 = (bf16[192,2,256]{2,1,0:T(2,128)(2,1)}, bf16[192,2,256]{2,1,0:T(2,128)(2,1)S(1)}, u32[]{:S(2)}) copy-start(bf16[192,2,256]{2,1,0:T(2,128)(2,1)S(1)} %reshape.267) | copy-start | bytes 589828
  101.6 55.7 %copy-start.35 = (bf16[192,2,128]{2,0,1:T(8,128)(2,1)}, bf16[192,2,128]{2,0,1:T(8,128)(2,1)S(1)}, u32[]{:S(2)}) copy-start(bf16[192,2,128]{2,0,1:T(8,128)(2,1)S(1)} %get-tuple-element.121) | copy-start | bytes 294916
  101.6 55.7 %copy-start.37 = (bf16[192,2,128]{2,0,1:T(8,128)(2,1)}, bf16[192,2,128]{2,0,1:T(8,128)(2,1)S(1)}, u32[]{:S(2)}) copy-start(bf16[192,2,128]{2,0,1:T(8,128)(2,1)S(1)} %get-tuple-element.122) | copy-start | bytes 294916
  157.2 1.1 copy-start.31
  157.3 1.1 copy-start.32
  157.9 54.3 %copy-start.45 = (f32[2,2,192]{2,1,0:T(2,128)}, f32[2,2,192]{2,1,0:T(2,128)S(1)}, u32[]{:S(2)}) copy-start(f32[2,2,192]{2,1,0:T(2,128)S(1)} %log_add_fusion) | copy-start | bytes 9220
  159.2 53.0 %copy-start.19 = (bf16[192,1024]{1,0:T(8,128)(2,1)}, bf16[192,1024]{1,0:T(8,128)(2,1)S(1)}, u32[]{:S(2)}) copy-start(bf16[192,1024]{1,0:T(8,128)(2,1)S(1)} %convert_element_type.109) | copy-start | bytes 1179652
  212.2 28.4 %copy-start.1 = (bf16[96,2304]{1,0:T(8,128)(2,1)S(1)}, bf16[96,2304]{1,0:T(8,128)(2,1)}, u32[]{:S(2)}) copy-start(bf16[96,2304]{1,0:T(8,128)(2,1)} %param.14) | copy-start | bytes 1327108
  212.3 138.5 %all-gather.23.cloned.1.call-start = ((), (), s32[]{:S(2)}) async-start(), calls=%async_computation.11 | async-start | bytes 22560768 | tf_op jit(solution)/shard_map/all_gather | solution.py:130
  212.8 249.6 %all-gather.25.cloned.1.call-start = ((), (), s32[]{:S(2)}) async-start(), calls=%async_computation.12 | async-start | bytes 22560768 | tf_op jit(solution)/shard_map/all_gather | solution.py:131
  213.6 360.4 %all-gather.27.cloned.1.call-start = ((), (), s32[]{:S(2)}) async-start(), calls=%async_computation.13 | async-start | bytes 22560768 | tf_op jit(solution)/shard_map/all_gather | solution.py:132
  214.3 400.8 %reduce-scatter.11.cloned.1.call-start = ((), (), s32[]{:S(2)}) async-start(), calls=%async_computation.14 | async-start | bytes 2654208 | tf_op jit(solution)/shard_map/reduce_scatter | solution.py:187
  214.4 27.8 %copy-start.33 = (f32[2304]{0:T(1024)}, f32[2304]{0:T(1024)S(1)}, u32[]{:S(2)}) copy-start(f32[2304]{0:T(1024)S(1)} %convert_element_type.111) | copy-start | bytes 27652
  240.6 1.6 copy-start.43
  255.1 207.4 %copy-start.8 = (bf16[192,2304]{1,0:T(8,128)(2,1)}, bf16[192,2304]{1,0:T(8,128)(2,1)S(1)}, u32[]{:S(2)}) copy-start(bf16[192,2304]{1,0:T(8,128)(2,1)S(1)} %all_gather.74) | copy-start | bytes 2654212
  574.0 42.5 %copy-start.7 = (bf16[96,2304]{1,0:T(8,128)(2,1)S(1)}, bf16[96,2304]{1,0:T(8,128)(2,1)}, u32[]{:S(2)}) copy-start(bf16[96,2304]{1,0:T(8,128)(2,1)} %param.27) | copy-start | bytes 1327108
  586.7 144.3 %all-gather.29.cloned.1.call-start = ((), (), s32[]{:S(2)}) async-start(), calls=%async_computation.15 | async-start | bytes 22560768 | tf_op jit(solution)/shard_map/all_gather | solution.py:216
  620.8 221.8 %all-gather.31.cloned.1.call-start = ((), (), s32[]{:S(2)}) async-start(), calls=%async_computation.16 | async-start | bytes 22560768 | tf_op jit(solution)/shard_map/all_gather | solution.py:214
  621.5 332.5 %all-gather.33.cloned.1.call-start = ((), (), s32[]{:S(2)}) async-start(), calls=%async_computation.17 | async-start | bytes 22560768 | tf_op jit(solution)/shard_map/all_gather | solution.py:215
  622.1 373.6 %reduce-scatter.13.cloned.1.call-start = ((), (), s32[]{:S(2)}) async-start(), calls=%async_computation.18 | async-start | bytes 2654208 | tf_op jit(solution)/shard_map/reduce_scatter | solution.py:239
  635.1 110.1 %copy-start.5 = (bf16[192,2304]{1,0:T(8,128)(2,1)}, bf16[192,2304]{1,0:T(8,128)(2,1)S(1)}, u32[]{:S(2)}) copy-start(bf16[192,2304]{1,0:T(8,128)(2,1)S(1)} %all_gather.79) | copy-start | bytes 2654212
  954.1 41.6 %copy-start.34 = (f32[2304]{0:T(1024)S(1)}, f32[2304]{0:T(1024)}, u32[]{:S(2)}) copy-start(f32[2304]{0:T(1024)} %copy-done.33) | copy-start | bytes 27652
  967.2 30.5 %copy-start = (f32[96,2304]{1,0:T(8,128)S(1)}, f32[96,2304]{1,0:T(8,128)}, u32[]{:S(2)}) copy-start(f32[96,2304]{1,0:T(8,128)} %reduce-scatter.9.cloned.1.call-done) | copy-start | bytes 2654212
  967.2 30.5 %copy-start.44 = (f32[96]{0:T(128)S(1)}, f32[96]{0:T(128)}, u32[]{:S(2)}) copy-start(f32[96]{0:T(128)} %copy-done.43) | copy-start | bytes 1156
  967.2 83.7 %all-gather.35.cloned.1.call-start = ((), (), s32[]{:S(2)}) async-start(), calls=%async_computation.19 | async-start | bytes 5013504 | tf_op jit(solution)/shard_map/all_gather | solution.py:213
  967.8 137.0 %all-gather.37.cloned.1.call-start = ((), (), s32[]{:S(2)}) async-start(), calls=%async_computation.20 | async-start | bytes 5013504 | tf_op jit(solution)/shard_map/all_gather | solution.py:210
  968.4 179.4 %all-gather.39.cloned.1.call-start = ((), (), s32[]{:S(2)}) async-start(), calls=%async_computation.21 | async-start | bytes 2506752 | tf_op jit(solution)/shard_map/all_gather | solution.py:211
  969.0 222.0 %all-gather.41.cloned.1.call-start = ((), (), s32[]{:S(2)}) async-start(), calls=%async_computation.22 | async-start | bytes 2506752 | tf_op jit(solution)/shard_map/all_gather | solution.py:212
  969.6 418.8 %reduce-scatter.15.cloned.1.call-start = ((), (), s32[]{:S(2)}) async-start(), calls=%async_computation.23 | async-start | bytes 1327104 | tf_op jit(solution)/shard_map/reduce_scatter | solution.py:310
  1013.4 43.0 %copy-start.24 = (f32[2,192,192,2]{2,1,3,0:T(8,128)S(1)}, f32[2,192,192,2]{2,1,3,0:T(8,128)}, u32[]{:S(2)}) copy-start(f32[2,192,192,2]{2,1,3,0:T(8,128)} %copy-done.23) | copy-start | bytes 1769476
  1013.4 43.0 %copy-start.30 = (pred[192,192]{0,1:T(8,128)(4,1)S(1)}, pred[192,192]{0,1:T(8,128)(4,1)}, u32[]{:S(2)}) copy-start(pred[192,192]{0,1:T(8,128)(4,1)} %copy-done.29) | copy-start | bytes 110596
  1013.4 43.0 %copy-start.46 = (f32[2,2,192]{2,1,0:T(2,128)S(1)}, f32[2,2,192]{2,1,0:T(2,128)}, u32[]{:S(2)}) copy-start(f32[2,2,192]{2,1,0:T(2,128)} %copy-done.45) | copy-start | bytes 9220
  1013.4 44.2 %copy-start.26 = (bf16[192,2,256]{2,1,0:T(2,128)(2,1)S(1)}, bf16[192,2,256]{2,1,0:T(2,128)(2,1)}, u32[]{:S(2)}) copy-start(bf16[192,2,256]{2,1,0:T(2,128)(2,1)} %copy-done.25) | copy-start | bytes 589828
  1056.4 4.7 copy-start.11
  1056.5 4.7 copy-start.13
  1056.9 5.1 copy-start.36
  1067.1 43.0 %copy-start.21 = (bf16[24,8,4,256]{3,1,2,0:T(8,128)(2,1)}, bf16[24,8,4,256]{3,1,2,0:T(8,128)(2,1)S(1)}, u32[]{:S(2)}) copy-start(bf16[24,8,4,256]{3,1,2,0:T(8,128)(2,1)S(1)} %copy.123) | copy-start | bytes 1179652
  1147.8 3.2 copy-start.20
  1151.1 5.0 copy-start.14
  1151.1 5.0 copy-start.16
  1151.1 5.0 copy-start.22
  1156.1 34.9 %copy-start.15 = (bf16[2,24,8,256]{3,2,0,1:T(8,128)(2,1)S(1)}, bf16[2,24,8,256]{3,2,0,1:T(8,128)(2,1)}, u32[]{:S(2)}) copy-start(bf16[2,24,8,256]{3,2,0,1:T(8,128)(2,1)} %copy.122) | copy-start | bytes 589828
  1194.6 318.4 %reduce-scatter.19.cloned.1.call-start = ((), (), s32[]{:S(2)}) async-start(), calls=%async_computation.25 | async-start | bytes 30081024
  1241.2 1.2 copy-start.6
  1241.2 28.9 %copy-start.9 = (bf16[192,2304]{1,0:T(8,128)(2,1)S(1)}, bf16[192,2304]{1,0:T(8,128)(2,1)}, u32[]{:S(2)}) copy-start(bf16[192,2304]{1,0:T(8,128)(2,1)} %copy-done.8) | copy-start | bytes 2654212
  1241.2 28.9 %copy-start.17 = (bf16[192,4608]{1,0:T(8,128)(2,1)S(1)}, bf16[192,4608]{1,0:T(8,128)(2,1)}, u32[]{:S(2)}) copy-start(bf16[192,4608]{1,0:T(8,128)(2,1)} %get-tuple-element.105) | copy-start | bytes 5308420
  1241.2 1453.5 %reduce-scatter.17.cloned.1.call-start = ((), (), s32[]{:S(2)}) async-start(), calls=%async_computation.24 | async-start | bytes 135364608 | tf_op jit(solution)/shard_map/reduce_scatter | solution.py:229
  1242.3 27.8 %copy-start.18 = (bf16[192,4608]{1,0:T(8,128)(2,1)S(1)}, bf16[192,4608]{1,0:T(8,128)(2,1)}, u32[]{:S(2)}) copy-start(bf16[192,4608]{1,0:T(8,128)(2,1)} %get-tuple-element.106) | copy-start | bytes 5308420
  1388.3 1.0 copy-start.28
  1388.3 2.4 copy-start.38
  1388.3 2.4 copy-start.39
  1388.3 2.4 copy-start.40
  1388.3 45.4 %copy-start.4 = (f32[96,2304]{1,0:T(8,128)S(1)}, f32[96,2304]{1,0:T(8,128)}, u32[]{:S(2)}) copy-start(f32[96,2304]{1,0:T(8,128)} %copy-done.3) | copy-start | bytes 2654212
  (4 other events, 3.8 us)
Sparse Core Ops, SparseCore 0:
  10.3 45.2 all-gather.16
  57.8 41.0 all-gather.14
  101.3 51.8 all-gather.18
  155.3 51.6 all-gather.20
  212.4 26.8 reduce-scatter.8
  240.7 110.0 all-gather.22
  352.4 109.9 all-gather.24
  464.0 109.9 all-gather.26
  586.8 28.2 reduce-scatter.10
  620.9 109.9 all-gather.28
  732.6 109.9 all-gather.30
  844.0 109.9 all-gather.32
  967.3 28.2 reduce-scatter.12
  997.8 53.1 all-gather.34
  1053.1 51.6 all-gather.36
  1106.9 40.8 all-gather.38
  1150.0 41.0 all-gather.40
  1194.7 17.3 reduce-scatter.14
  1241.3 271.5 reduce-scatter.18
  1517.0 1177.6 reduce-scatter.16
where the time goes:
time: 2720 us; the launch traced here: 2710 us
  waiting for transfers between devices  2170 us (80%)
  matrix products  189 us (7%)
  blocking collectives  151 us (6%)
  other arithmetic  127 us (5%)
  local copies, waits for them, and re-layouts  54.3 us (2%)
    reduce_scatter x1, waiting for transfers between devices, shards(): lax.psum_scatter(jnp.concatenate([contract_first(left_rows, gate_up_grad)...  1180 us
    all_gather x1, waiting for transfers between devices, shards(): lax.all_gather(up_weight, 'fsdp', axis=0, tiled=True)  100 us
    all_gather x1, waiting for transfers between devices, shards(): lax.all_gather(held_back[5], 'fsdp', axis=0, tiled=True)  98.8 us
    all_gather x1, waiting for transfers between devices, shards(): lax.all_gather(held_back[4], 'fsdp', axis=0, tiled=True)  97.4 us
    all_gather x1, waiting for transfers between devices, shards(): lax.all_gather(down_weight, 'fsdp', axis=0, tiled=True)  96.9 us
    all_gather x1, waiting for transfers between devices, shards(): lax.all_gather(held_back[6], 'fsdp', axis=0, tiled=True)  95.9 us
    all_gather x1, waiting for transfers between devices, shards(): lax.all_gather(gate_weight, 'fsdp', axis=0, tiled=True)  95.7 us
    concatenate x1, other arithmetic, shards(): jnp.concatenate([contract_first(left_rows, gate_up_grad), contract_first(...  85.6 us
  transfers between devices with their start and end apart: 20, of which 18 were waited for; matrix products, arithmetic and copies ran while one was open for 12% of the time, Pallas kernels for 0%

commit v1 on v0

--- a/solution.py
+++ b/solution.py
@@ -8,6 +8,25 @@
 EPSILON = 1e-06
 SOFTCAP = 50.0
 NEGATIVE = -1e30
+
+
+def advance_the_plane(x_in):
+    axis_name = "fsdp"
+    e_next = lax.axis_size(axis_name)
+    taken_in = lax.axis_index(axis_name)
+    p_next, val = (e_next, taken_in)
+    out_arr, big = (x_in, 1)
+    while big < p_next:
+        x_next = lax.ppermute(
+            out_arr,
+            axis_name=axis_name,
+            perm=list(map(lambda dev_i: (dev_i, dev_i ^ big), range(p_next))),
+        )
+        block_last = jnp.concatenate([out_arr, x_next], axis=0)
+        a_next = jnp.concatenate([x_next, out_arr], axis=0)
+        out_arr = jnp.where(val & big == 0, block_last, a_next)
+        big = 2 * big
+    return out_arr
 
 
 def contract_last(left_rows, right_rows):
@@ -213,7 +232,7 @@
         lax.all_gather(held_back[3], "fsdp", axis=0, tiled=True),
         lax.all_gather(held_back[4], "fsdp", axis=0, tiled=True),
         lax.all_gather(held_back[5], "fsdp", axis=0, tiled=True),
-        lax.all_gather(held_back[6], "fsdp", axis=0, tiled=True),
+        advance_the_plane(held_back[6]),
     )
     branch_two_grad = held_back[7]
     feed_grad_rows = lax.all_gather(branch_two_grad, "tp", axis=0, tiled=True)

time: 2720 us -> 3230 us (1.19)
  waiting for transfers between devices: 2170 us -> 2650 us
    ppermute x0 -> x4, waiting for transfers between devices: none -> 778 us  [advance_the_plane(): lax.ppermute(out_arr, axis_name=axis_name, perm=list(map(lambda dev_i: (d...]
    all_gather x1, waiting for transfers between devices: 98.8 us -> 0.01 us  [shards(): lax.all_gather(held_back[5], 'fsdp', axis=0, tiled=True)]
    all_gather x1, waiting for transfers between devices: 97.4 us -> 0.01 us  [shards(): lax.all_gather(held_back[4], 'fsdp', axis=0, tiled=True)]
    all_gather x1 -> x0, waiting for transfers between devices: 95.9 us -> none  [shards(): lax.all_gather(held_back[6], 'fsdp', axis=0, tiled=True)]
    unnamed x21 -> x20, waiting for transfers between devices: 84.9 us -> 85.7 us
  transfers between devices with their start and end apart: 20 -> 23, of which waited for: 18 -> 19; matrix products, arithmetic and copies ran while one was open for 12% -> 11% of each run, Pallas kernels for 0% -> 0%
where the time goes in v1:
time: 3230 us; the launch traced here: 3220 us
  waiting for transfers between devices  2650 us (82%)
  matrix products  195 us (6%)
  blocking collectives  150 us (5%)
  other arithmetic  149 us (5%)
  local copies, waits for them, and re-layouts  53.5 us (2%)
    reduce_scatter x1, waiting for transfers between devices, shards(): lax.psum_scatter(jnp.concatenate([contract_first(left_rows, gate_up_grad)...  1180 us
    ppermute x4, waiting for transfers between devices, advance_the_plane(): lax.ppermute(out_arr, axis_name=axis_name, perm=list(map(lambda dev_i: (d...  778 us
    all_gather x1, waiting for transfers between devices, shards(): lax.all_gather(up_weight, 'fsdp', axis=0, tiled=True)  100 us
    all_gather x1, waiting for transfers between devices, shards(): lax.all_gather(down_weight, 'fsdp', axis=0, tiled=True)  96.9 us
    all_gather x1, waiting for transfers between devices, shards(): lax.all_gather(gate_weight, 'fsdp', axis=0, tiled=True)  95.9 us
    unnamed x20, waiting for transfers between devices  85.7 us
    concatenate x1, other arithmetic, shards(): jnp.concatenate([contract_first(left_rows, gate_up_grad), contract_first(...  85.1 us
    dot_general x4, matrix products, contract_first(): lax.dot_general(left_rows, right_rows, (((0,), (0,)), ((), ())), preferre...  73.4 us
  transfers between devices with their start and end apart: 23, of which 19 were waited for; matrix products, arithmetic and copies ran while one was open for 11% of the time, Pallas kernels for 0%

profile of v1, /device:TPU:0, one launch (start us, length us, event | category | flops | bytes accessed | tf_op | source)
XLA Modules:
  0.0 3224.3 jit_solution(6757925401088185730)
XLA Ops:
  15.4 63.9 %all-reduce.5 = (bf16[2304]{0:T(1024)(128)(2,1)S(1)}, bf16[2304]{0:T(1024)(128)(2,1)S(1)}, bf16[2304]{0:T(1024)(128)(2,1)S(1)}, bf16[2304]{0:T(1024)(128)(2,1)S(1)}) all-reduce(bf16[2304]{0:T(1024)(128)(2,1)S(1)} %dynamic-update-slice, bf16[2304]{0:T(1024)(128)(2,1)S(1)} %dynamic-update-slice.1, ...), channel_id=1, replica_groups=mesh['fsdp'=16,'tp'=2] {'fsdp'}, use_global_device_ids=true, to_apply=%add | all-reduce | flops 9216 | bytes 36864
  83.3 9.0 all_gather.64
  93.0 2.3 fusion.115
  95.6 3.4 all-gather.14.cloned.1.call-done
  99.0 2.3 convolution_convert_fusion.2
  101.6 51.6 %all-gather.18.cloned.1.call-done = bf16[2304,1024]{1,0:T(8,128)(2,1)} async-done(((bf16[144,1024]{1,0:T(8,128)(2,1)}), bf16[2304,1024]{1,0:T(8,128)(2,1)}) %all-gather.18.cloned.1.call-update) | async-done | bytes 4718608 | tf_op jit(solution)/shard_map/all_gather | solution.py:141
  153.2 3.4 fusion.116
  159.3 47.7 %all-gather.20.cloned.1.call-done = bf16[2304,1024]{1,0:T(8,128)(2,1)} async-done(((bf16[144,1024]{1,0:T(8,128)(2,1)}), bf16[2304,1024]{1,0:T(8,128)(2,1)}) %all-gather.20.cloned.1.call-update) | async-done | bytes 4718608 | tf_op jit(solution)/shard_map/all_gather | solution.py:144
  207.0 5.2 fusion.117
  214.4 24.9 reduce-scatter.9.cloned.1.call-done
  239.3 1.3 multiply_reduce_fusion.6
  240.7 1.5 multiply_reduce_fusion.5
  242.3 12.6 all_gather.71
  254.9 95.9 %all-gather.22.cloned.1.call-done = bf16[2304,4608]{1,0:T(8,128)(2,1)} async-done(((bf16[144,4608]{1,0:T(8,128)(2,1)}), bf16[2304,4608]{1,0:T(8,128)(2,1)}) %all-gather.22.cloned.1.call-update) | async-done | bytes 21233680 | tf_op jit(solution)/shard_map/all_gather | solution.py:149
  350.8 11.4 fusion.118
  362.2 100.3 %all-gather.24.cloned.1.call-done = bf16[2304,4608]{1,0:T(8,128)(2,1)} async-done(((bf16[144,4608]{1,0:T(8,128)(2,1)}), bf16[2304,4608]{1,0:T(8,128)(2,1)}) %all-gather.24.cloned.1.call-update) | async-done | bytes 21233680 | tf_op jit(solution)/shard_map/all_gather | solution.py:150
  462.4 14.7 multiply_convert_fusion.1
  477.2 96.9 %all-gather.26.cloned.1.call-done = bf16[2304,4608]{1,0:T(8,128)(2,1)} async-done(((bf16[144,4608]{1,0:T(8,128)(2,1)}), bf16[2304,4608]{1,0:T(8,128)(2,1)}) %all-gather.26.cloned.1.call-update) | async-done | bytes 21233680 | tf_op jit(solution)/shard_map/all_gather | solution.py:151
  574.0 12.6 fusion.119
  586.8 28.4 reduce-scatter.11.cloned.1.call-done
  616.5 2.1 fusion.45
  618.7 2.4 fusion.38
  622.0 3.2 collective-permute-done
  625.1 3.1 maximum_select_fusion.4
  628.2 1.5 collective-permute-start.1
  629.8 115.7 %collective-permute-done.1 = bf16[288,4608]{1,0:T(8,128)(2,1)} collective-permute-done((bf16[288,4608]{1,0:T(8,128)(2,1)S(1)}, bf16[288,4608]{1,0:T(8,128)(2,1)}, u32[]{:S(2)}, u32[]{:S(2)}) %collective-permute-start.1) | collective-permute-done | bytes 2654240 | tf_op jit(solution)/shard_map/ppermute | solution.py:20
  745.4 6.4 maximum_select_fusion.3
  751.8 215.7 %collective-permute-done.2 = bf16[576,4608]{1,0:T(8,128)(2,1)} collective-permute-done((bf16[576,4608]{1,0:T(8,128)(2,1)}, bf16[576,4608]{1,0:T(8,128)(2,1)}, u32[]{:S(2)}, u32[]{:S(2)}) %collective-permute-start.2) | collective-permute-done | bytes 5308448 | tf_op jit(solution)/shard_map/ppermute | solution.py:20
  967.6 12.6 maximum_select_fusion.2
  980.2 4.3 collective-permute-start.3
  984.5 11.0 all_gather.76
  995.4 443.8 %collective-permute-done.3 = bf16[1152,4608]{1,0:T(8,128)(2,1)} collective-permute-done((bf16[1152,4608]{1,0:T(8,128)(2,1)}, bf16[1152,4608]{1,0:T(8,128)(2,1)}, u32[]{:S(2)}, u32[]{:S(2)}) %collective-permute-start.3) | collective-permute-done | bytes 10616864 | tf_op jit(solution)/shard_map/ppermute | solution.py:20
  1439.3 19.5 multiply_convert_fusion
  1458.8 13.2 fusion.120
  1472.0 13.1 convolution_add_fusion.2
  1487.7 23.9 reduce-scatter.13.cloned.1.call-done
  1511.6 2.0 multiply_reduce_fusion
  1513.6 2.2 multiply_reduce_fusion.1
  1516.8 12.8 all_gather.79
  1529.6 37.4 %all-gather.32.cloned.1.call-done = bf16[2304,1024]{1,0:T(8,128)(2,1)} async-done(((bf16[144,1024]{1,0:T(8,128)(2,1)}), bf16[2304,1024]{1,0:T(8,128)(2,1)}) %all-gather.32.cloned.1.call-update) | async-done | bytes 4718608 | tf_op jit(solution)/shard_map/all_gather | solution.py:232
  1567.0 4.2 convolution_convert_fusion
  1574.8 2.3 convolution_bitcast_fusion.2
  1577.9 3.0 fusion.46
  1583.0 37.9 %all-gather.34.cloned.1.call-done = bf16[2304,1024]{1,0:T(8,128)(2,1)} async-done(((bf16[144,1024]{1,0:T(8,128)(2,1)}), bf16[2304,1024]{1,0:T(8,128)(2,1)}) %all-gather.34.cloned.1.call-update) | async-done | bytes 4718608 | tf_op jit(solution)/shard_map/all_gather | solution.py:229
  1620.9 5.2 fusion.121
  1626.1 37.8 %all-gather.36.cloned.1.call-done = bf16[2304,512]{1,0:T(8,128)(2,1)} async-done(((bf16[144,512]{1,0:T(8,128)(2,1)}), bf16[2304,512]{1,0:T(8,128)(2,1)}) %all-gather.36.cloned.1.call-update) | async-done | bytes 2359312 | tf_op jit(solution)/shard_map/all_gather | solution.py:230
  1663.9 3.2 convolution_add_fusion.1
  1667.2 5.0 fusion.122
  1672.2 8.0 fusion.51
  1680.2 26.9 all-gather.38.cloned.1.call-done
  1707.1 3.5 fusion.8
  1710.7 18.9 pad_maximum_fusion.1
  1729.6 27.7 copy.111
  1757.6 27.1 fusion.123
  1784.7 33.3 %fusion.16 = f32[2304,9216]{1,0:T(8,128)} fusion(bf16[192,2304]{1,0:T(8,128)(2,1)S(1)} %copy-done.11, bf16[192,4608]{1,0:T(8,128)(2,1)S(1)} %copy-done.21, bf16[192,4608]{1,0:T(8,128)(2,1)S(1)} %copy-done.22), kind=kOutput, calls=%fused_computation.26 | convolution fusion | flops 8160804864 | bytes 89358336 | tf_op jit(solution)/shard_map/dot_general | solution.py:39
  1817.9 85.1 %pad_maximum_fusion = f32[2304,13824]{1,0:T(8,128)} fusion(f32[2304,4608]{1,0:T(8,128)} %fusion.123, f32[2304,9216]{1,0:T(8,128)} %fusion.16), kind=kLoop, calls=%fused_computation.1 | loop fusion | flops 31850496 | bytes 254803968 | tf_op jit(solution)/shard_map/concatenate | solution.py:249
  1904.0 1.4 fusion.43
  1905.5 40.6 %all-reduce.4 = (f32[2304]{0:T(1024)S(1)}, f32[2304]{0:T(1024)S(1)}, f32[2304]{0:T(1024)S(1)}, f32[2304]{0:T(1024)S(1)}) all-reduce(f32[2304]{0:T(1024)S(1)} %get-tuple-element.87, f32[2304]{0:T(1024)S(1)} %copy-done.44, f32[2304]{0:T(1024)S(1)} %copy-done.43, f32[2304]{0:T(1024)S(1)} %copy-done.42), channel_id=1, replica_groups=mesh['fsdp'=16,'tp'=2] {'fsdp','tp'}, use_global_device_ids=true, to_apply=%region_19.20 | all-reduce | flops 9216 | bytes 73728 | tf_op jit(solution)/shard_map/psum | solution.py:339
  1948.6 2.2 fusion.40
  1950.9 78.1 %reduce-scatter.19.cloned.1.call-done = f32[144,3072]{1,0:T(8,128)} async-done(((f32[2304,3072]{1,0:T(8,128)}), f32[144,3072]{1,0:T(8,128)}) %reduce-scatter.19.cloned.1.call-update) | async-done | bytes 1769488
  2029.0 1.9 fusion.112
  2030.9 2.4 fusion.111
  2033.3 1177.5 %reduce-scatter.17.cloned.1.call-done = f32[144,13824]{1,0:T(8,128)} async-done(((f32[2304,13824]{1,0:T(8,128)}), f32[144,13824]{1,0:T(8,128)}) %reduce-scatter.17.cloned.1.call-update) | async-done | bytes 7962640 | tf_op jit(solution)/shard_map/reduce_scatter | solution.py:248
  3210.8 6.8 fusion.110
  (212 shorter events, 33.4 us)
Async XLA Ops:
  7.2 85.1 %copy-start.51 = (s32[1,9]{1,0:T(1,128)S(1)}, s32[1,9]{1,0:T(1,128)}, u32[]{:S(2)}) copy-start(s32[1,9]{1,0:T(1,128)} %param.15) | copy-start | bytes 112
  7.2 85.8 %all-gather.16.cloned.1.call-start = ((), (), s32[]{:S(2)}) async-start(), calls=%async_computation.7 | async-start | bytes 2506752 | tf_op jit(solution)/shard_map/all_gather | solution.py:142
  7.9 91.1 %all-gather.14.cloned.1.call-start = ((), (), s32[]{:S(2)}) async-start(), calls=%async_computation.6 | async-start | bytes 2506752 | tf_op jit(solution)/shard_map/all_gather | solution.py:143
  8.7 144.5 %all-gather.18.cloned.1.call-start = ((), (), s32[]{:S(2)}) async-start(), calls=%async_computation.8 | async-start | bytes 5013504 | tf_op jit(solution)/shard_map/all_gather | solution.py:141
  9.4 197.6 %all-gather.20.cloned.1.call-start = ((), (), s32[]{:S(2)}) async-start(), calls=%async_computation.9 | async-start | bytes 5013504 | tf_op jit(solution)/shard_map/all_gather | solution.py:144
  10.0 229.3 %reduce-scatter.9.cloned.1.call-start = ((), (), s32[]{:S(2)}) async-start(), calls=%async_computation.10 | async-start | bytes 2654208 | tf_op jit(solution)/shard_map/reduce_scatter | solution.py:194
  82.1 13.5 copy-start.45
  92.3 60.9 %copy-start.3 = (bf16[192,2304]{1,0:T(8,128)(2,1)}, bf16[192,2304]{1,0:T(8,128)(2,1)S(1)}, u32[]{:S(2)}) copy-start(bf16[192,2304]{1,0:T(8,128)(2,1)S(1)} %all_gather.64) | copy-start | bytes 2654212
  92.5 65.5 %copy-start.33 = (pred[192,192]{0,1:T(8,128)(4,1)}, pred[192,192]{0,1:T(8,128)(4,1)S(1)}, u32[]{:S(2)}) copy-start(pred[192,192]{0,1:T(8,128)(4,1)S(1)} %fusion.84) | copy-start | bytes 110596
  92.9 64.0 %copy-start.12 = (f32[192,128]{1,0:T(8,128)}, f32[192,128]{1,0:T(8,128)S(1)}, u32[]{:S(2)}) copy-start(f32[192,128]{1,0:T(8,128)S(1)} %get-tuple-element.125) | copy-start | bytes 294916
  92.9 64.0 %copy-start.14 = (f32[192,128]{1,0:T(8,128)}, f32[192,128]{1,0:T(8,128)S(1)}, u32[]{:S(2)}) copy-start(f32[192,128]{1,0:T(8,128)S(1)} %get-tuple-element.126) | copy-start | bytes 294916
  101.3 56.7 %copy-start.29 = (bf16[192,2,256]{2,1,0:T(2,128)(2,1)}, bf16[192,2,256]{2,1,0:T(2,128)(2,1)S(1)}, u32[]{:S(2)}) copy-start(bf16[192,2,256]{2,1,0:T(2,128)(2,1)S(1)} %reshape.267) | copy-start | bytes 589828
  101.6 55.7 %copy-start.39 = (bf16[192,2,128]{2,0,1:T(8,128)(2,1)}, bf16[192,2,128]{2,0,1:T(8,128)(2,1)S(1)}, u32[]{:S(2)}) copy-start(bf16[192,2,128]{2,0,1:T(8,128)(2,1)S(1)} %get-tuple-element.121) | copy-start | bytes 294916
  101.6 55.7 %copy-start.41 = (bf16[192,2,128]{2,0,1:T(8,128)(2,1)}, bf16[192,2,128]{2,0,1:T(8,128)(2,1)S(1)}, u32[]{:S(2)}) copy-start(bf16[192,2,128]{2,0,1:T(8,128)(2,1)S(1)} %get-tuple-element.122) | copy-start | bytes 294916
  157.2 49.8 %copy-start.35 = (bf16[192,4,128]{2,0,1:T(8,128)(2,1)}, bf16[192,4,128]{2,0,1:T(8,128)(2,1)S(1)}, u32[]{:S(2)}) copy-start(bf16[192,4,128]{2,0,1:T(8,128)(2,1)S(1)} %copy.83) | copy-start | bytes 589828
  158.0 54.3 %copy-start.49 = (f32[2,2,192]{2,1,0:T(2,128)}, f32[2,2,192]{2,1,0:T(2,128)S(1)}, u32[]{:S(2)}) copy-start(f32[2,2,192]{2,1,0:T(2,128)S(1)} %log_add_fusion) | copy-start | bytes 9220
  159.3 53.0 %copy-start.23 = (bf16[192,1024]{1,0:T(8,128)(2,1)}, bf16[192,1024]{1,0:T(8,128)(2,1)S(1)}, u32[]{:S(2)}) copy-start(bf16[192,1024]{1,0:T(8,128)(2,1)S(1)} %convert_element_type.109) | copy-start | bytes 1179652
  212.3 28.4 copy-start.1
  212.3 138.5 %all-gather.22.cloned.1.call-start = ((), (), s32[]{:S(2)}) async-start(), calls=%async_computation.11 | async-start | bytes 22560768 | tf_op jit(solution)/shard_map/all_gather | solution.py:149
  212.9 249.6 %all-gather.24.cloned.1.call-start = ((), (), s32[]{:S(2)}) async-start(), calls=%async_computation.12 | async-start | bytes 22560768 | tf_op jit(solution)/shard_map/all_gather | solution.py:150
  213.6 360.4 %all-gather.26.cloned.1.call-start = ((), (), s32[]{:S(2)}) async-start(), calls=%async_computation.13 | async-start | bytes 22560768 | tf_op jit(solution)/shard_map/all_gather | solution.py:151
  214.4 400.8 %reduce-scatter.11.cloned.1.call-start = ((), (), s32[]{:S(2)}) async-start(), calls=%async_computation.14 | async-start | bytes 2654208 | tf_op jit(solution)/shard_map/reduce_scatter | solution.py:206
  214.4 27.8 copy-start.37
  240.6 121.5 %copy-start.47 = (f32[96]{0:T(128)}, f32[96]{0:T(128)S(1)}, u32[]{:S(2)}) copy-start(f32[96]{0:T(128)S(1)} %add_rsqrt_fusion.2) | copy-start | bytes 1156
  254.9 207.5 %copy-start.10 = (bf16[192,2304]{1,0:T(8,128)(2,1)}, bf16[192,2304]{1,0:T(8,128)(2,1)S(1)}, u32[]{:S(2)}) copy-start(bf16[192,2304]{1,0:T(8,128)(2,1)S(1)} %all_gather.71) | copy-start | bytes 2654212
  574.0 42.5 %copy-start.8 = (bf16[96,2304]{1,0:T(8,128)(2,1)S(1)}, bf16[96,2304]{1,0:T(8,128)(2,1)}, u32[]{:S(2)}) copy-start(bf16[96,2304]{1,0:T(8,128)(2,1)} %param.27) | copy-start | bytes 1327108
  586.7 872.1 %all-gather.28.cloned.1.call-start = ((), (), s32[]{:S(2)}) async-start(), calls=%async_computation.15 | async-start | bytes 22560768 | tf_op jit(solution)/shard_map/all_gather | solution.py:233
  616.5 5.3 copy-start.7
  621.1 850.9 %all-gather.30.cloned.1.call-start = ((), (), s32[]{:S(2)}) async-start(), calls=%async_computation.16 | async-start | bytes 22560768 | tf_op jit(solution)/shard_map/all_gather | solution.py:234
  621.8 889.8 %reduce-scatter.13.cloned.1.call-start = ((), (), s32[]{:S(2)}) async-start(), calls=%async_computation.17 | async-start | bytes 2654208 | tf_op jit(solution)/shard_map/reduce_scatter | solution.py:258
  621.9 3.3 collective-permute-start
  628.2 117.2 %collective-permute-start.1 = (bf16[288,4608]{1,0:T(8,128)(2,1)S(1)}, bf16[288,4608]{1,0:T(8,128)(2,1)}, u32[]{:S(2)}, u32[]{:S(2)}) collective-permute-start(bf16[288,4608]{1,0:T(8,128)(2,1)S(1)} %maximum_select_fusion.4), channel_id=1, source_target_pairs={{0,4},{2,6},{4,0},{6,2},{8,12},{10,14},{12,8},{14,10},{16,20},{18,... | collective-permute-start | bytes 7962632 | tf_op jit(solution)/shard_map/ppermute | solution.py:20
  751.8 215.7 %collective-permute-start.2 = (bf16[576,4608]{1,0:T(8,128)(2,1)}, bf16[576,4608]{1,0:T(8,128)(2,1)}, u32[]{:S(2)}, u32[]{:S(2)}) collective-permute-start(bf16[576,4608]{1,0:T(8,128)(2,1)} %maximum_select_fusion.3), channel_id=1, source_target_pairs={{0,8},{2,10},{4,12},{6,14},{8,0},{10,2},{12,4},{14,6},{16,24},{18,... | collective-permute-start | bytes 15925256 | tf_op jit(solution)/shard_map/ppermute | solution.py:20
  751.8 232.6 %copy-start.19 = (bf16[96,2304]{1,0:T(8,128)(2,1)S(1)}, bf16[96,2304]{1,0:T(8,128)(2,1)}, u32[]{:S(2)}) copy-start(bf16[96,2304]{1,0:T(8,128)(2,1)} %get-tuple-element.21) | copy-start | bytes 1327108
  980.2 459.1 %collective-permute-start.3 = (bf16[1152,4608]{1,0:T(8,128)(2,1)}, bf16[1152,4608]{1,0:T(8,128)(2,1)}, u32[]{:S(2)}, u32[]{:S(2)}) collective-permute-start(bf16[1152,4608]{1,0:T(8,128)(2,1)} %maximum_select_fusion.2), channel_id=1, source_target_pairs={{0,16},{2,18},{4,20},{6,22},{8,24},{10,26},{12,28},{14,30},{16,0},... | collective-permute-start | bytes 31850504 | tf_op jit(solution)/shard_map/ppermute | solution.py:20
  1458.8 13.2 copy-start.20
  1485.1 28.5 copy-start
  1485.1 28.5 copy-start.9
  1485.1 28.5 copy-start.38
  1485.1 28.5 copy-start.48
  1485.1 81.9 %all-gather.32.cloned.1.call-start = ((), (), s32[]{:S(2)}) async-start(), calls=%async_computation.18 | async-start | bytes 5013504 | tf_op jit(solution)/shard_map/all_gather | solution.py:232
  1485.9 135.0 %all-gather.34.cloned.1.call-start = ((), (), s32[]{:S(2)}) async-start(), calls=%async_computation.19 | async-start | bytes 5013504 | tf_op jit(solution)/shard_map/all_gather | solution.py:229
  1486.5 177.5 %all-gather.36.cloned.1.call-start = ((), (), s32[]{:S(2)}) async-start(), calls=%async_computation.20 | async-start | bytes 2506752 | tf_op jit(solution)/shard_map/all_gather | solution.py:230
  1487.0 220.1 %all-gather.38.cloned.1.call-start = ((), (), s32[]{:S(2)}) async-start(), calls=%async_computation.21 | async-start | bytes 2506752 | tf_op jit(solution)/shard_map/all_gather | solution.py:231
  1487.6 415.5 %reduce-scatter.15.cloned.1.call-start = ((), (), s32[]{:S(2)}) async-start(), calls=%async_computation.22 | async-start | bytes 1327104 | tf_op jit(solution)/shard_map/reduce_scatter | solution.py:329
  1529.6 42.9 %copy-start.28 = (f32[2,192,192,2]{2,1,3,0:T(8,128)S(1)}, f32[2,192,192,2]{2,1,3,0:T(8,128)}, u32[]{:S(2)}) copy-start(f32[2,192,192,2]{2,1,3,0:T(8,128)} %copy-done.27) | copy-start | bytes 1769476
  1529.6 42.9 %copy-start.34 = (pred[192,192]{0,1:T(8,128)(4,1)S(1)}, pred[192,192]{0,1:T(8,128)(4,1)}, u32[]{:S(2)}) copy-start(pred[192,192]{0,1:T(8,128)(4,1)} %copy-done.33) | copy-start | bytes 110596
  1529.6 42.9 %copy-start.50 = (f32[2,2,192]{2,1,0:T(2,128)S(1)}, f32[2,2,192]{2,1,0:T(2,128)}, u32[]{:S(2)}) copy-start(f32[2,2,192]{2,1,0:T(2,128)} %copy-done.49) | copy-start | bytes 9220
  1529.6 44.0 %copy-start.30 = (bf16[192,2,256]{2,1,0:T(2,128)(2,1)S(1)}, bf16[192,2,256]{2,1,0:T(2,128)(2,1)}, u32[]{:S(2)}) copy-start(bf16[192,2,256]{2,1,0:T(2,128)(2,1)} %copy-done.29) | copy-start | bytes 589828
  1572.5 4.6 copy-start.13
  1572.5 4.6 copy-start.15
  1573.0 5.0 copy-start.40
  1582.9 43.2 %copy-start.25 = (bf16[24,8,4,256]{3,1,2,0:T(8,128)(2,1)}, bf16[24,8,4,256]{3,1,2,0:T(8,128)(2,1)S(1)}, u32[]{:S(2)}) copy-start(bf16[24,8,4,256]{3,1,2,0:T(8,128)(2,1)S(1)} %copy.123) | copy-start | bytes 1179652
  1667.1 5.0 copy-start.4
  1667.2 5.0 copy-start.16
  1667.2 5.0 copy-start.18
  1667.2 5.0 copy-start.26
  1672.2 34.9 %copy-start.17 = (bf16[2,24,8,256]{3,2,0,1:T(8,128)(2,1)S(1)}, bf16[2,24,8,256]{3,2,0,1:T(8,128)(2,1)}, u32[]{:S(2)}) copy-start(bf16[2,24,8,256]{3,2,0,1:T(8,128)(2,1)} %copy.122) | copy-start | bytes 589828
  1710.6 318.4 %reduce-scatter.19.cloned.1.call-start = ((), (), s32[]{:S(2)}) async-start(), calls=%async_computation.24 | async-start | bytes 30081024
  1757.3 27.3 copy-start.11
  1757.3 27.3 copy-start.21
  1757.3 1453.4 %reduce-scatter.17.cloned.1.call-start = ((), (), s32[]{:S(2)}) async-start(), calls=%async_computation.23 | async-start | bytes 135364608 | tf_op jit(solution)/shard_map/reduce_scatter | solution.py:248
  1757.6 27.1 copy-start.22
  1903.0 45.6 %copy-start.6 = (f32[96,2304]{1,0:T(8,128)S(1)}, f32[96,2304]{1,0:T(8,128)}, u32[]{:S(2)}) copy-start(f32[96,2304]{1,0:T(8,128)} %copy-done.5) | copy-start | bytes 2654212
  (11 other events, 19.0 us)
Sparse Core Ops, SparseCore 0:
  10.3 45.2 all-gather.15
  57.8 41.0 all-gather.13
  101.3 51.8 all-gather.17
  155.3 51.6 all-gather.19
  212.4 26.8 reduce-scatter.8
  240.7 110.0 all-gather.21
  352.4 109.9 all-gather.23
  464.0 109.9 all-gather.25
  586.8 28.3 reduce-scatter.10
  621.2 179.7 all-gather.27
  802.6 191.8 all-gather.29
  1485.2 26.3 reduce-scatter.12
  1513.9 53.1 all-gather.31
  1569.2 51.6 all-gather.33
  1623.0 40.8 all-gather.35
  1666.0 41.0 all-gather.37
  1710.8 17.3 reduce-scatter.14
  1757.4 271.5 reduce-scatter.18
  2033.2 1177.4 reduce-scatter.16
